TPU v7x, 32 devices: a whole 2x2x4 slice. The times are simulated.
32 devices in a mesh: dp: 2 (over x), tp: 4 (over z), ep: 4 (over y, core).
Axes of the slice: x: 2, y: 2, z: 4, core: 2. Of those that a mesh axis runs over, the one named last changes fastest.
Arguments:
- tokens_in: bfloat16 [4096, 2048], P(('dp', 'ep', 'tp')), parts along dimension 0
- expert_ids: int32 [4096, 8], P(('dp', 'ep', 'tp')), parts along dimension 0
- router_gates: float32 [4096, 8], P(('dp', 'ep', 'tp')), parts along dimension 0
- w_gate: bfloat16 [128, 2048, 768], P('ep', None, 'tp')
- w_up: bfloat16 [128, 2048, 768], P('ep', None, 'tp')
- w_down: bfloat16 [128, 768, 2048], P('ep', 'tp')
Outputs:
- output: bfloat16 [4096, 2048], P(('dp', 'ep', 'tp')), parts along dimension 0
There are 2 independent parts. A program takes and returns all parts, laid end to end along the dimension named above; an argument that names none is the same for every part.
All inputs are finite; a program needn't handle non-finite values.
Results may differ from a plain program's by a relative error of at most 0.0012.
Values are sent between devices in bfloat16 or wider.
A program may use at most 1 GiB of HBM per device.

v0:
```python
import jax
import jax.numpy as jnp
from jax import lax
from jax.sharding import PartitionSpec as P

TOKEN_AXES = ('dp', 'ep', 'tp')
GROUP_AXES = ('ep', 'tp')


def solution(mesh):
    groups = mesh.shape['ep']

    def expert_block(tok_shard, id_shard, gate_shard, w_gate, w_up, w_down):
        tok_group = lax.all_gather(tok_shard, GROUP_AXES, axis=0, tiled=True)
        id_group = lax.all_gather(id_shard, GROUP_AXES, axis=0, tiled=True)
        gate_group = lax.all_gather(gate_shard, GROUP_AXES, axis=0, tiled=True)
        tok_count, choices = id_group.shape
        local_count = w_gate.shape[0]
        pair_slots = tok_count * choices // groups
        local_exp = id_group.reshape(-1) - lax.axis_index('ep') * local_count
        sort_key = jnp.where((local_exp >= 0) & (local_exp < local_count), local_exp, local_count)
        sort_order = jnp.argsort(sort_key, stable=True)[:pair_slots]
        group_sizes = jnp.bincount(sort_key, length=local_count + 1)[:local_count].astype(jnp.int32)
        row_ids = sort_order // choices
        is_local = sort_key[sort_order] < local_count
        gate_rows = gate_group.reshape(-1)[sort_order]
        tok_rows = tok_group[row_ids]
        h_gate = lax.ragged_dot(tok_rows, w_gate, group_sizes, preferred_element_type=jnp.float32)
        h_up = lax.ragged_dot(tok_rows, w_up, group_sizes, preferred_element_type=jnp.float32)
        hidden = (jax.nn.silu(h_gate) * h_up).astype(jnp.bfloat16)
        out_rows = lax.ragged_dot(hidden, w_down, group_sizes, preferred_element_type=jnp.float32)
        weighted = jnp.where(is_local[:, None], out_rows * gate_rows[:, None], 0.0)
        partial_out = jax.ops.segment_sum(weighted, row_ids, num_segments=tok_count)
        y_shard = lax.psum_scatter(partial_out, GROUP_AXES, scatter_dimension=0, tiled=True)
        return y_shard.astype(jnp.bfloat16)

    return jax.shard_map(
        expert_block,
        mesh=mesh,
        in_specs=(P(TOKEN_AXES, None), P(TOKEN_AXES, None), P(TOKEN_AXES, None),
                  P('ep', None, 'tp'), P('ep', None, 'tp'), P('ep', 'tp', None)),
        out_specs=P(TOKEN_AXES, None),
        check_vma=False,
    )
```

profile of v0, /device:TPU:0, one launch (start us, length us, event | category | flops | bytes accessed | tf_op | source)
XLA Modules:
  0.0 748.3 jit_solution(11731523130002131153)
XLA Ops:
  6.5 0.0 copy-start
  6.5 0.0 all-gather.2.cloned.1.call-start
  6.5 0.7 all-gather.2.cloned.1.call-update
  7.3 0.0 reduce-scatter.2.cloned.1.call-start
  7.3 35.3 %all_gather.9 = s32[2048,8]{0,1:T(8,128)S(1)} all-gather(s32[128,8]{0,1:T(8,128)} %param.7), channel_id=1, replica_groups=mesh['dp'=2,'tp'=4,'ep'=4] {'ep','tp'}, dimensions={0}, use_global_device_ids=true | all-gather | bytes 69632 | tf_op jit(solution)/shard_map/all_gather | solution.py:15
  42.6 0.3 copy.9
  43.0 0.5 sub.29
  43.5 0.5 sub.27
  44.0 0.1 fusion.7
  44.1 113.9 %scatter_custom_fusion = s32[33]{0:T(128)} fusion(s32[16384]{0:T(1024)S(1)} %bitcast.2, s32[16384]{0:T(1024)S(1)} %broadcast.70, s32[]{:T(128)} %constant.14.clone.1), kind=kCustom, calls=%fused_computation.29 | custom fusion | flops 16384 | bytes 136 | tf_op jit(solution)/shard_map/scatter-add | solution.py:23
  158.1 2.5 ragged-dot-metadata
  160.6 7.8 %sort.17 = (s32[16384]{0:T(1024)}, s32[16384]{0:T(1024)S(1)}) sort(s32[16384]{0:T(1024)S(1)} %and_select_fusion.1, s32[16384]{0:T(1024)S(1)} %iota.4), dimensions={0}, to_apply=%region_0.1 | sort | flops 229376 | bytes 262144 | tf_op jit(solution)/shard_map/jit(argsort)/sort | solution.py:22
  168.4 23.0 %gather_fusion = s32[4096]{0:T(1024)S(1)} fusion(s32[16384]{0:T(1024)S(1)} %and_select_fusion.1, s32[4096]{0:T(1024)S(1)} %get-tuple-element.19), kind=kCustom, calls=%fused_computation | custom fusion | bytes 49152 | tf_op jit(solution)/shard_map/gather | solution.py:25
  191.4 0.0 copy-done
  191.4 29.1 %all_gather.11 = f32[2048,8]{0,1:T(8,128)S(1)} all-gather(f32[128,8]{0,1:T(8,128)S(1)} %copy-done), channel_id=1, replica_groups=mesh['dp'=2,'tp'=4,'ep'=4] {'ep','tp'}, dimensions={0}, use_global_device_ids=true | all-gather | bytes 69632 | tf_op jit(solution)/shard_map/all_gather | solution.py:16
  220.5 0.3 copy.13
  220.8 0.5 reshape.37
  221.3 23.0 %gather_fusion.2 = f32[4096]{0:T(1024)S(1)} fusion(f32[16384]{0:T(1024)S(1)} %reshape.37, s32[4096]{0:T(1024)S(1)} %get-tuple-element.19), kind=kCustom, calls=%fused_computation.2 | custom fusion | bytes 49152 | tf_op jit(solution)/shard_map/gather | solution.py:26
  244.4 37.9 %copy.11 = bf16[32,2048,192]{2,1,0:T(8,128)(2,1)} copy(bf16[32,2048,192]{1,2,0:T(8,128)(2,1)} %param.9) | data formatting | bytes 50331648 | tf_op args[3]
  282.3 37.9 %copy.12 = bf16[32,2048,192]{2,1,0:T(8,128)(2,1)} copy(bf16[32,2048,192]{1,2,0:T(8,128)(2,1)} %param.10) | data formatting | bytes 50331648 | tf_op args[4]
  320.2 0.0 all-gather.2.cloned.1.call-done
  320.2 35.8 %gather_fusion.1 = bf16[4096,2048]{1,0:T(8,128)(2,1)} fusion(bf16[2048,2048]{1,0:T(8,128)(2,1)} %all-gather.2.cloned.1.call-done, s32[4096]{0:T(1024)S(1)} %get-tuple-element.20), kind=kCustom, calls=%fused_computation.1 | custom fusion | bytes 33570816 | tf_op jit(solution)/shard_map/gather | solution.py:27
  356.0 45.5 %ragged-dot-none.2 = f32[4096,192]{1,0:T(8,128)} custom-call(s32[1]{0:T(128)} %get-tuple-element.7, s32[33]{0:T(128)} %get-tuple-element.8, s32[47]{0:T(128)} %get-tuple-element.9, s32[47]{0:T(128)} %get-tuple-element.10, s32[1]{0:T(128)} %get-tuple-element.7, bf16[4096,2048]{1,0:T(8,128)(2,1)} %gather_fusion.1, bf16[32,2048,192]{2,1,0:T(8,128)(2,1)} %copy.11), custom_call_target="tpu_custom_call" | custom-call | flops 3221225472 | bytes 45088896 | tf_op jit(solution)/shard_map/ragged_dot_general/ragged-dot-none
  401.5 45.5 %ragged-dot-none.1 = f32[4096,192]{1,0:T(8,128)} custom-call(s32[1]{0:T(128)} %get-tuple-element.7, s32[33]{0:T(128)} %get-tuple-element.8, s32[47]{0:T(128)} %get-tuple-element.9, s32[47]{0:T(128)} %get-tuple-element.10, s32[1]{0:T(128)} %get-tuple-element.7, bf16[4096,2048]{1,0:T(8,128)(2,1)} %gather_fusion.1, bf16[32,2048,192]{2,1,0:T(8,128)(2,1)} %copy.12), custom_call_target="tpu_custom_call" | custom-call | flops 3221225472 | bytes 45088896 | tf_op jit(solution)/shard_map/ragged_dot_general/ragged-dot-none
  447.0 6.0 multiply_convert_fusion
  452.9 49.8 %ragged-dot-none = f32[4096,2048]{1,0:T(8,128)} custom-call(s32[1]{0:T(128)} %get-tuple-element.7, s32[33]{0:T(128)} %get-tuple-element.8, s32[47]{0:T(128)} %get-tuple-element.9, s32[47]{0:T(128)} %get-tuple-element.10, s32[1]{0:T(128)} %get-tuple-element.7, bf16[4096,192]{1,0:T(8,128)(2,1)} %multiply_convert_fusion, bf16[32,192,2048]{2,1,0:T(8,128)(2,1)} %param.11), custom_call_target="tpu_custom_call" | custom-call | flops 3221225472 | bytes 60293248 | tf_op jit(solution)/shard_map/ragged_dot_general/ragged-dot-none
  502.7 62.3 %scatter_custom_fusion.1 = f32[2048,2048]{1,0:T(8,128)} fusion(s32[4096]{0:T(1024)S(1)} %get-tuple-element.21, f32[4096,2048]{1,0:T(8,128)} %ragged-dot-none, f32[]{:T(128)} %constant.11.clone.1, f32[4096]{0:T(1024)S(1)} %gather_fusion.2, pred[4096]{0:T(1024)(128)(4,1)S(1)} %broadcast_compare_fusion), kind=kCustom, calls=%fused_computation.5 | custom fusion | flops 25165824 | bytes 50353152 | tf_op jit(solution)/shard_map/scatter-add | solution.py:33
  565.0 0.0 reduce-scatter.2.cloned.1.call-update
  565.1 174.3 %reduce-scatter.2.cloned.1.call-done = f32[128,2048]{1,0:T(8,128)} async-done(((f32[2048,2048]{1,0:T(8,128)}), f32[128,2048]{1,0:T(8,128)}) %reduce-scatter.2.cloned.1.call-update) | async-done | bytes 1048592 | tf_op jit(solution)/shard_map/reduce_scatter | solution.py:34
  739.4 2.1 convert_element_type.7
  (6 shorter events, 0.1 us)
Async XLA Ops:
  6.5 184.9 %copy-start = (f32[128,8]{0,1:T(8,128)S(1)}, f32[128,8]{0,1:T(8,128)}, u32[]{:S(2)}) copy-start(f32[128,8]{0,1:T(8,128)} %param.8) | copy-start | bytes 12292
  6.5 313.6 %all-gather.2.cloned.1.call-start = ((), (), s32[]{:S(2)}) async-start(), calls=%async_computation.1 | async-start | bytes 8912896 | tf_op jit(solution)/shard_map/all_gather | solution.py:14
  7.3 732.1 %reduce-scatter.2.cloned.1.call-start = ((), (), s32[]{:S(2)}) async-start(), calls=%async_computation.2 | async-start | bytes 17825792 | tf_op jit(solution)/shard_map/reduce_scatter | solution.py:34
Sparse Core Ops, SparseCore 0:
  9.5 78.1 all-gather.1
  565.2 174.1 reduce-scatter.1
where the time goes:
time: 753 us; the launch traced here: 748 us
  other arithmetic  192 us (25%)
  waiting for transfers between devices  175 us (23%)
  local copies, waits for them, and re-layouts  160 us (21%)
  Pallas kernels  143 us (19%)
  blocking collectives  64.4 us (9%)
  between operations  13.5 us (2%)
    reduce_scatter x1, waiting for transfers between devices, expert_block(): lax.psum_scatter(partial_out, GROUP_AXES, scatter_dimension=0, tiled=True)  174 us
    another operation x3, Pallas kernels  141 us
    scatter-add x1, other arithmetic, expert_block(): jnp.bincount(sort_key, length=local_count + 1)[:local_count]  114 us
    unnamed x4, local copies, waits for them, and re-layouts  75.8 us
    scatter-add x1, other arithmetic, expert_block(): partial_out = jax.ops.segment_sum(weighted, row_ids, num_segments=tok_count)  62.3 us
    gather x1, local copies, waits for them, and re-layouts, expert_block(): tok_rows = tok_group[row_ids]  35.8 us
    all_gather x1, blocking collectives, expert_block(): id_group = lax.all_gather(id_shard, GROUP_AXES, axis=0, tiled=True)  35.3 us
    all_gather x1, blocking collectives, expert_block(): gate_group = lax.all_gather(gate_shard, GROUP_AXES, axis=0, tiled=True)  29.1 us
  transfers between devices with their start and end apart: 2, of which 1 were waited for; matrix products, arithmetic and copies ran while one was open for 33% of the time, Pallas kernels for 0%

commit v1 on v0

v1 whole, which is shorter than its diff:
```python
import jax
import jax.numpy as jnp
from jax import lax
from jax.experimental import pallas as pl
from jax.experimental.pallas import tpu as pltpu
from jax.sharding import PartitionSpec as P

TOKEN_AXES = ('dp', 'ep', 'tp')
GROUP_AXES = ('ep', 'tp')
MB = 192
NBUF = 4
LANES = 128


def _moe_kernel(n_tok, dim, ffp, n_exp, n_pairs,
                tok_ref, gate_ref, start_ref, x_hbm, wg_hbm, wu_hbm, w2_hbm, y_hbm,
                xf, xst, yacc, wbuf, w2buf, xe, xb, obuf, xsem, wsem, ysem):
    cbs = dim // LANES
    tile_rows = cbs * 8
    xc = xst.shape[1]
    n_xc = n_tok // xc

    def w_copies(e, slot):
        return (pltpu.make_async_copy(wg_hbm.at[e], wbuf.at[slot, pl.ds(0, ffp)], wsem.at[slot, 0]),
                pltpu.make_async_copy(wu_hbm.at[e], wbuf.at[slot, pl.ds(ffp, ffp)], wsem.at[slot, 1]),
                pltpu.make_async_copy(w2_hbm.at[e], w2buf.at[slot], wsem.at[slot, 2]))

    def x_copy(i, slot):
        return pltpu.make_async_copy(x_hbm.at[pl.ds(i * xc, xc)], xst.at[slot], xsem.at[slot])

    x_copy(0, 0).start()
    x_copy(1, 1).start()
    for e in range(NBUF - 1):
        for c in w_copies(e, e):
            c.start()

    zero = jnp.zeros((tile_rows, LANES), jnp.float32)

    def x_chunk(i, carry):
        slot = lax.rem(i, 2)
        x_copy(i, slot).wait()

        def conv(r, carry2):
            r16 = pl.multiple_of(r * 16, 16)
            row = pl.multiple_of((i * xc + r16) * cbs, 2 * tile_rows)
            for cb in range(cbs):
                v = xst[slot, pl.ds(r16, 16), pl.ds(cb * LANES, LANES)].astype(jnp.float32)
                xf[pl.ds(row + cb * 8, 8), :] = v[:8]
                xf[pl.ds(row + tile_rows + cb * 8, 8), :] = v[8:]
            yacc[pl.ds(row, tile_rows), :] = zero
            yacc[pl.ds(row + tile_rows, tile_rows), :] = zero
            return carry2

        lax.fori_loop(0, xc // 16, conv, 0)

        @pl.when(i + 2 < n_xc)
        def _():
            x_copy(i + 2, slot).start()
        return carry

    lax.fori_loop(0, n_xc, x_chunk, 0)

    def expert(e, carry):
        slot = lax.rem(e, NBUF)

        @pl.when(e + NBUF - 1 < n_exp)
        def _():
            for c in w_copies(e + NBUF - 1, lax.rem(e + NBUF - 1, NBUF)):
                c.start()

        first = start_ref[e]
        last = start_ref[e + 1]
        for c in w_copies(e, slot):
            c.wait()

        def block(b, carry2):
            base = first + b * MB
            n = jnp.minimum(last - base, MB)
            groups = (n + 7) // 8

            def gather(m, c3):
                row = pl.multiple_of(m * tile_rows, tile_rows)
                vals = []
                for k in range(8):
                    t = tok_ref[base + m * 8 + k]
                    src = (t >> 3) * tile_rows + (t & 7)
                    vals.append(xf[pl.ds(src, cbs, stride=8), :])
                for k in range(8):
                    xe[pl.ds(row + k, cbs, stride=8), :] = vals[k]
                return c3

            lax.fori_loop(0, groups, gather, 0)

            def conv(r, c3):
                row = pl.multiple_of(r * 2 * tile_rows, 2 * tile_rows)
                for cb in range(cbs):
                    v = jnp.concatenate([xe[pl.ds(row + cb * 8, 8), :],
                                         xe[pl.ds(row + tile_rows + cb * 8, 8), :]], axis=0)
                    xb[pl.ds(pl.multiple_of(r * 16, 16), 16), pl.ds(cb * LANES, LANES)] = v.astype(jnp.bfloat16)
                return c3

            lax.fori_loop(0, (n + 15) // 16, conv, 0)

            at = lax.dot_general(wbuf[slot], xb[...], (((1,), (1,)), ((), ())),
                                 preferred_element_type=jnp.float32)
            ht = jax.nn.silu(at[:ffp]) * at[ffp:]
            h = ht.T.astype(jnp.bfloat16)
            for nc in range(dim // 256):
                o = jnp.dot(h, w2buf[slot, :, pl.ds(nc * 256, 256)], preferred_element_type=jnp.float32)
                for rb in range(MB // 8):
                    for s in range(2):
                        obuf[pl.ds(rb * tile_rows + (nc * 2 + s) * 8, 8), :] = (
                            o[rb * 8:rb * 8 + 8, s * LANES:(s + 1) * LANES])

            def combine(m, c3):
                row = pl.multiple_of(m * tile_rows, tile_rows)
                dst, acc = [], []
                for k in range(8):
                    p = m * 8 + k
                    t = jnp.where(p < n, tok_ref[base + p], n_tok)
                    d = pl.multiple_of(t * cbs, cbs)
                    dst.append(d)
                    acc.append(yacc[pl.ds(d, cbs), :]
                               + obuf[pl.ds(row + k, cbs, stride=8), :] * gate_ref[base + p])
                for k in range(8):
                    yacc[pl.ds(dst[k], cbs), :] = acc[k]
                return c3

            lax.fori_loop(0, groups, combine, 0)
            return carry2

        lax.fori_loop(0, (last - first + MB - 1) // MB, block, 0)
        return carry

    lax.fori_loop(0, n_exp, expert, 0)
    out = pltpu.make_async_copy(yacc.at[pl.ds(0, n_tok * cbs)], y_hbm, ysem)
    out.start()
    out.wait()


def _moe(tok, gate, start, x, wgt, wut, w2):
    n_exp, ffp, dim = wgt.shape
    n_tok = x.shape[0]
    cbs = dim // LANES
    import functools
    smem = pl.BlockSpec(memory_space=pltpu.SMEM)
    hbm = pl.BlockSpec(memory_space=pl.ANY)
    return pl.pallas_call(
        functools.partial(_moe_kernel, n_tok, dim, ffp, n_exp, tok.shape[0]),
        out_shape=jax.ShapeDtypeStruct((n_tok * cbs, LANES), jnp.float32),
        in_specs=[smem, smem, smem, hbm, hbm, hbm, hbm],
        out_specs=hbm,
        scratch_shapes=[
            pltpu.VMEM((n_tok * cbs, LANES), jnp.float32),
            pltpu.VMEM((2, 128, dim), jnp.bfloat16),
            pltpu.VMEM(((n_tok + 8) * cbs, LANES), jnp.float32),
            pltpu.VMEM((NBUF, 2 * ffp, dim), jnp.bfloat16),
            pltpu.VMEM((NBUF, ffp, dim), jnp.bfloat16),
            pltpu.VMEM((MB * cbs, LANES), jnp.float32),
            pltpu.VMEM((MB, dim), jnp.bfloat16),
            pltpu.VMEM((MB * cbs, LANES), jnp.float32),
            pltpu.SemaphoreType.DMA((2,)),
            pltpu.SemaphoreType.DMA((NBUF, 3)),
            pltpu.SemaphoreType.DMA,
        ],
        compiler_params=pltpu.CompilerParams(vmem_limit_bytes=62 * 1024 * 1024),
        cost_estimate=pl.CostEstimate(flops=20_000_000_000, bytes_accessed=100_000_000, transcendentals=1_000_000),
    )(tok, gate, start, x, wgt, wut, w2)


def _routing(ids, gates, local_count, first_expert):
    devs, choices, rows = ids.shape
    n_tok = devs * rows
    tok = (lax.broadcasted_iota(jnp.int32, ids.shape, 0) * rows
           + lax.broadcasted_iota(jnp.int32, ids.shape, 2))
    local = ids - first_expert
    key = jnp.where((local >= 0) & (local < local_count), local * n_tok + tok, local_count * n_tok)
    key = key.reshape(-1)
    n_pairs = key.shape[0] // 4
    bounds = jnp.arange(local_count + 1, dtype=jnp.int32) * n_tok
    start = jnp.sum((key[None, :] < bounds[:, None]).astype(jnp.int32), axis=1)
    key_s, gate_s = lax.sort((key, gates.reshape(-1)), num_keys=1, is_stable=False)
    tok_s = key_s[:n_pairs + MB] & (n_tok - 1)
    return tok_s, gate_s[:n_pairs + MB], start


def solution(mesh):
    def expert_block(tok_shard, id_shard, gate_shard, w_gate, w_up, w_down):
        x = lax.all_gather(tok_shard, GROUP_AXES, axis=0, tiled=True)
        meta = jnp.concatenate([id_shard.T.astype(jnp.float32), gate_shard.T], axis=0)
        meta = lax.all_gather(meta, GROUP_AXES, axis=0)
        choices = id_shard.shape[1]
        ids = meta[:, :choices].astype(jnp.int32)
        gates = meta[:, choices:]
        local_count = w_gate.shape[0]
        tok, gate, start = _routing(ids, gates, local_count, lax.axis_index('ep') * local_count)
        y = _moe(tok, gate, start, x, jnp.swapaxes(w_gate, 1, 2), jnp.swapaxes(w_up, 1, 2), w_down)
        y = lax.psum_scatter(y, GROUP_AXES, scatter_dimension=0, tiled=True)
        return y.reshape(tok_shard.shape).astype(jnp.bfloat16)

    return jax.shard_map(
        expert_block,
        mesh=mesh,
        in_specs=(P(TOKEN_AXES, None), P(TOKEN_AXES, None), P(TOKEN_AXES, None),
                  P('ep', None, 'tp'), P('ep', None, 'tp'), P('ep', 'tp', None)),
        out_specs=P(TOKEN_AXES, None),
        check_vma=False,
    )
```

time: 753 us -> 373 us (0.50)
  other arithmetic: 192 us -> 10.9 us
  local copies, waits for them, and re-layouts: 160 us -> 1.62 us
  Pallas kernels: 143 us -> 99.2 us
  waiting for transfers between devices: 175 us -> 210 us
  blocking collectives: 64.4 us -> 36.5 us
    scatter-add x2 -> x0, other arithmetic: 176 us -> none  [the longest x1 114 us: expert_block(): jnp.bincount(sort_key, length=local_count + 1)[:local_count]]
    another operation x3 -> x0, Pallas kernels: 141 us -> none
    pallas_call x0 -> x1, Pallas kernels: none -> 99.2 us  [_moe(): pl.pallas_call(functools.partial(_moe_kernel, n_tok, dim, ffp, n_exp, tok...]
    gather x3 -> x0, local copies, waits for them, and re-layouts: 81.9 us -> none  [the longest x1 35.8 us: expert_block(): tok_rows = tok_group[row_ids]]
    unnamed x4 -> x0, local copies, waits for them, and re-layouts: 75.8 us -> none
    all_gather x1, waiting for transfers between devices: 0.02 us -> 35.1 us  [expert_block(): x = lax.all_gather(tok_shard, GROUP_AXES, axis=0, tiled=True)]
    all_gather x2 -> x1, blocking collectives: 64.4 us -> 36.5 us  [expert_block(): meta = lax.all_gather(meta, GROUP_AXES, axis=0)]
  transfers between devices with their start and end apart: 2 -> 2, of which waited for: 1 -> 2; matrix products, arithmetic and copies ran while one was open for 33% -> 3% of each run, Pallas kernels for 0% -> 0%
where the time goes in v1:
time: 373 us; the launch traced here: 372 us
  waiting for transfers between devices  210 us (56%)
  Pallas kernels  99.2 us (27%)
  blocking collectives  36.5 us (10%)
  between operations  13.4 us (4%)
  other arithmetic  10.9 us (3%)
    reduce_scatter x1, waiting for transfers between devices, expert_block(): y = lax.psum_scatter(y, GROUP_AXES, scatter_dimension=0, tiled=True)  175 us
    pallas_call x1, Pallas kernels, _moe(): pl.pallas_call(functools.partial(_moe_kernel, n_tok, dim, ffp, n_exp, tok...  99.2 us
    all_gather x1, blocking collectives, expert_block(): meta = lax.all_gather(meta, GROUP_AXES, axis=0)  36.5 us
    all_gather x1, waiting for transfers between devices, expert_block(): x = lax.all_gather(tok_shard, GROUP_AXES, axis=0, tiled=True)  35.1 us
  transfers between devices with their start and end apart: 2, of which 2 were waited for; matrix products, arithmetic and copies ran while one was open for 3% of the time, Pallas kernels for 0%

profile of v1, /device:TPU:0, one launch (start us, length us, event | category | flops | bytes accessed | tf_op | source)
XLA Modules:
  0.0 372.2 jit_solution(11823604509518499400)
XLA Ops:
  6.5 0.0 all-gather.3.cloned.1.call-start
  6.5 0.7 all-gather.3.cloned.1.call-update
  7.3 0.0 reduce-scatter.2.cloned.1.call-start
  7.3 0.7 convert_bitcast_fusion
  8.0 0.7 pad_maximum_fusion
  8.7 36.5 %all-gather = f32[256,128]{1,0:T(8,128)S(1)} all-gather(f32[16,128]{1,0:T(8,128)S(1)} %pad_maximum_fusion), channel_id=2, replica_groups=mesh['dp'=2,'tp'=4,'ep'=4] {'ep','tp'}, dimensions={0}, use_global_device_ids=true | all-gather | bytes 139264 | tf_op jit(solution)/shard_map/all_gather | solution.py:191
  45.2 0.1 select_bitcast_fusion
  45.3 6.4 %sort.15 = (s32[16384]{0:T(1024)S(1)}, f32[16384]{0:T(1024)S(1)}) sort(s32[16384]{0:T(1024)S(1)} %select_bitcast_fusion, f32[16384]{0:T(1024)S(1)} %slice_bitcast_fusion), dimensions={0}, to_apply=%region_0.1 | sort | flops 229376 | bytes 262144 | tf_op jit(solution)/shard_map/sort | solution.py:182
  51.7 0.6 slice.15.gate_ref
  52.4 1.1 convert_reduce_fusion.start_ref
  53.4 0.6 slice_and_fusion.tok_ref
  54.0 35.1 %all-gather.3.cloned.1.call-done.x_hbm = bf16[2048,2048]{1,0:T(8,128)(2,1)} async-done(((bf16[128,2048]{1,0:T(8,128)(2,1)}), bf16[2048,2048]{1,0:T(8,128)(2,1)}) %all-gather.3.cloned.1.call-update) | async-done | bytes 8388624 | tf_op jit(solution)/shard_map/all_gather | solution.py:189
  89.2 99.2 %shard_map.64 = f32[32768,128]{1,0:T(8,128)} custom-call(s32[4288]{0:T(1024)} %slice_and_fusion.tok_ref, f32[4288]{0:T(1024)} %slice.15.gate_ref, s32[33]{0:T(128)} %convert_reduce_fusion.start_ref, bf16[2048,2048]{1,0:T(8,128)(2,1)} %all-gather.3.cloned.1.call-done.x_hbm, bf16[32,192,2048]{2,1,0:T(8,128)(2,1)} %bitcast.10, bf16[32,192,2048]{2,1,0:T(8,128)(2,1)} %bitcast.11, ...), custom_call_target="tpu_custom_call" | custom-call | flops 20000000000 | bytes 100000000 | tf_op jit(solution)/shard_map/pallas_call | solution.py:148
  188.4 0.0 reduce-scatter.2.cloned.1.call-update
  188.4 174.6 %reduce-scatter.2.cloned.1.call-done = f32[2048,128]{1,0:T(8,128)} async-done(((f32[32768,128]{1,0:T(8,128)}), f32[2048,128]{1,0:T(8,128)}) %reduce-scatter.2.cloned.1.call-update) | async-done | bytes 1048592 | tf_op jit(solution)/shard_map/reduce_scatter | solution.py:198
  363.0 1.3 convert_element_type.22
  364.3 1.0 convert_element_type.23
  (3 shorter events, 0.0 us)
Async XLA Ops:
  6.5 82.6 %all-gather.3.cloned.1.call-start = ((), (), s32[]{:S(2)}) async-start(), calls=%async_computation.1 | async-start | bytes 8912896 | tf_op jit(solution)/shard_map/all_gather | solution.py:189
  7.3 355.8 %reduce-scatter.2.cloned.1.call-start = ((), (), s32[]{:S(2)}) async-start(), calls=%async_computation.2 | async-start | bytes 17825792 | tf_op jit(solution)/shard_map/reduce_scatter | solution.py:198
Sparse Core Ops, SparseCore 0:
  9.5 79.5 all-gather.2
  188.5 174.4 reduce-scatter.1

commit v2 on v1

--- a/solution.py
+++ b/solution.py
@@ -1,3 +1,5 @@
+import functools
+
 import jax
 import jax.numpy as jnp
 from jax import lax
@@ -142,7 +144,6 @@
     n_exp, ffp, dim = wgt.shape
     n_tok = x.shape[0]
     cbs = dim // LANES
-    import functools
     smem = pl.BlockSpec(memory_space=pltpu.SMEM)
     hbm = pl.BlockSpec(memory_space=pl.ANY)
     return pl.pallas_call(
@@ -184,19 +185,305 @@
     return tok_s, gate_s[:n_pairs + MB], start
 
 
+def _wire(ep, tp):
+    return ep // 2, ep % 2
+
+
+def _remote(src, dst, send, recv, ep, tp):
+    return pltpu.make_async_remote_copy(src_ref=src, dst_ref=dst, send_sem=send, recv_sem=recv,
+                                        device_id={'ep': ep, 'tp': tp},
+                                        device_id_type=pl.DeviceIdType.MESH)
+
+
+def _gather_kernel(tps, x_ref, meta_ref, xall, mall, buf, ms, mr, zs, zr, ys, yr, cs, cr, ls):
+    ep, tp = lax.axis_index('ep'), lax.axis_index('tp')
+    n_dev = mall.shape[0]
+    y, c = ep // 2, ep % 2
+    me = ep * tps + tp
+    partner = y * 2 + (1 - c)
+    across = (1 - y) * 2 + c
+
+    barrier = pltpu.get_barrier_semaphore()
+    for k in range(1, n_dev):
+        peer = (me + k) % n_dev
+        pl.semaphore_signal(barrier, inc=1, device_id={'ep': peer // tps, 'tp': peer % tps},
+                            device_id_type=pl.DeviceIdType.MESH)
+    pl.semaphore_wait(barrier, n_dev - 1)
+
+    metas = []
+    for k in range(1, n_dev):
+        peer = (me + k) % n_dev
+        cp = _remote(meta_ref, mall.at[me], ms.at[k], mr.at[k], peer // tps, peer % tps)
+        cp.start()
+        metas.append(cp)
+    mall[pl.ds(me, 1)] = meta_ref[...][None]
+
+    def body(z):
+        sends = []
+
+        def send(b, src, kind, ep_to, tp_to):
+            s, r = {'r': (zs, zr), 'l': (zs, zr), 'y': (ys, yr), 'c': (cs, cr)}[kind]
+            zi = b[1]
+            si = {'r': zi, 'l': tps + zi, 'y': zi, 'c': b[0] * tps + zi}[kind]
+            row = (b[0] if kind != 'c' else b[0])
+            idx = block(b)
+            cp = _remote(src, buf.at[idx], s.at[si], r.at[zi if kind in 'rly' else si], ep_to, tp_to)
+            cp.start()
+            sends.append(cp)
+
+        def block(b):
+            yy = y if b[0] == 0 else 1 - y
+            return (yy * 2 + c) * tps + b[1]
+
+        def keep(idx, src, n):
+            cp = pltpu.make_async_copy(src, xall.at[idx], ls.at[n])
+            cp.start()
+            locals_.append(cp)
+
+        locals_ = []
+        own = block((0, z))
+        if z < tps - 1:
+            send((0, z), x_ref, 'r', ep, z + 1)
+        if z > 0:
+            send((0, z), x_ref, 'l', ep, z - 1)
+        send((0, z), x_ref, 'y', across, z)
+        send((0, z), x_ref, 'c', partner, z)
+        keep(own, x_ref, 0)
+
+        events = []
+        order = [z]
+        for dist in range(1, tps):
+            if z - dist >= 0:
+                events.append((dist * 2, 'L', z - dist))
+                order.append(z - dist)
+            if z + dist < tps:
+                events.append((dist * 2, 'R', z + dist))
+                order.append(z + dist)
+        for i, zi in enumerate(order):
+            events.append((2 * i + 3, 'Y', zi))
+        events.sort(key=lambda t: t[0])
+        n = 1
+        for _, kind, zi in events:
+            if kind in 'LR':
+                b = (0, zi)
+                idx = block(b)
+                _remote(buf.at[idx], buf.at[idx], zs.at[zi], zr.at[zi], ep, z).wait_recv()
+                if kind == 'L' and z < tps - 1:
+                    send(b, buf.at[idx], 'r', ep, z + 1)
+                if kind == 'R' and z > 0:
+                    send(b, buf.at[idx], 'l', ep, z - 1)
+                send(b, buf.at[idx], 'y', across, z)
+            else:
+                b = (1, zi)
+                idx = block(b)
+                _remote(buf.at[idx], buf.at[idx], ys.at[zi], yr.at[zi], ep, z).wait_recv()
+            send(b, buf.at[idx], 'c', partner, z)
+            keep(idx, buf.at[idx], n)
+            n += 1
+        for same, zi in [(0, zi) for zi in order] + [(1, zi) for zi in order]:
+            yy = y if same == 0 else 1 - y
+            idx = (yy * 2 + (1 - c)) * tps + zi
+            _remote(buf.at[idx], buf.at[idx], cs.at[same * tps + zi], cr.at[same * tps + zi], ep, z).wait_recv()
+            keep(idx, buf.at[idx], n)
+            n += 1
+        for cp in sends:
+            cp.wait_send()
+        for cp in locals_:
+            cp.wait()
+
+    for z in range(tps):
+        @pl.when(tp == z)
+        def _(z=z):
+            body(z)
+
+    for cp in metas:
+        cp.wait_send()
+    for k in range(1, n_dev):
+        src = (me + n_dev - k) % n_dev
+        _remote(meta_ref, mall.at[src], ms.at[k], mr.at[k], ep, tp).wait_recv()
+
+
+def _gather(x, meta, n_dev, tps):
+    rows, dim = x.shape
+    vmem = pl.BlockSpec(memory_space=pltpu.VMEM)
+    dma = pltpu.SemaphoreType.DMA
+    return pl.pallas_call(
+        functools.partial(_gather_kernel, tps),
+        out_shape=(jax.ShapeDtypeStruct((n_dev, rows, dim), x.dtype),
+                   jax.ShapeDtypeStruct((n_dev,) + meta.shape, meta.dtype)),
+        in_specs=[vmem, vmem],
+        out_specs=(pl.BlockSpec(memory_space=pl.ANY), vmem),
+        scratch_shapes=[
+            pltpu.VMEM((n_dev, rows, dim), x.dtype),
+            dma((n_dev,)), dma((n_dev,)), dma((2 * tps,)), dma((tps,)), dma((tps,)), dma((tps,)),
+            dma((2 * tps,)), dma((2 * tps,)), dma((n_dev,)),
+        ],
+        compiler_params=pltpu.CompilerParams(collective_id=0, has_side_effects=True,
+                                             vmem_limit_bytes=48 * 1024 * 1024),
+    )(x, meta)
+
+
+NS = 2
+
+
+def _scatter_kernel(tps, p_hbm, out_ref, own, recd, recy, recr, recl, obuf,
+                    ds_, dr, ls, ys, yr, zs, rr, lr):
+    ep, tp = lax.axis_index('ep'), lax.axis_index('tp')
+    y, c = ep // 2, ep % 2
+    partner = y * 2 + (1 - c)
+    across = (1 - y) * 2 + c
+    rows, dim = out_ref.shape
+    cbs = dim // LANES
+    blk = rows * cbs
+    sub = blk // NS
+    step = min(256, sub)
+
+    barrier = pltpu.get_barrier_semaphore()
+
+    def sig(e, t):
+        pl.semaphore_signal(barrier, inc=1, device_id={'ep': e, 'tp': t}, device_id_type=pl.DeviceIdType.MESH)
+
+    def accumulate(dst, d0, *srcs):
+        @pl.loop(0, sub // step)
+        def _(i):
+            r = pl.multiple_of(i * step, step)
+            v = dst[pl.ds(pl.multiple_of(d0 + r, step), step), :]
+            for ref, s0 in srcs:
+                v = v + ref[pl.ds(pl.multiple_of(s0 + r, step), step), :]
+            dst[pl.ds(pl.multiple_of(d0 + r, step), step), :] = v
+
+    def body(z):
+        sig(partner, z)
+        sig(across, z)
+        if z > 0:
+            sig(ep, z - 1)
+        if z < tps - 1:
+            sig(ep, z + 1)
+        pl.semaphore_wait(barrier, 2 + (z > 0) + (z < tps - 1))
+
+        order = {0: [3, 2, 1, 0], 1: [3, 0, 2, 1], 2: [0, 3, 1, 2], 3: [0, 1, 2, 3]}[z]
+        sends = []
+        work = [(d, s) for d in order for s in range(NS)]
+
+        def off(half, d, s):
+            return (half * tps + d) * blk + s * sub
+
+        def sem_i(half, d, s):
+            return (half * tps + d) * NS + s
+
+        for half in range(2):
+            yy = (1 - y) if half == 0 else y
+            for d, s in work:
+                i = sem_i(half, d, s)
+                src = ((yy * 2 + (1 - c)) * tps + d) * blk + s * sub
+                cp = _remote(p_hbm.at[pl.ds(pl.multiple_of(src, sub), sub)], recd.at[pl.ds(off(half, d, s), sub)],
+                             ds_.at[i], dr.at[i], partner, z)
+                cp.start()
+                sends.append(cp)
+                src = ((yy * 2 + c) * tps + d) * blk + s * sub
+                pltpu.make_async_copy(p_hbm.at[pl.ds(pl.multiple_of(src, sub), sub)],
+                                      own.at[pl.ds(off(half, d, s), sub)], ls.at[i]).start()
+
+        def settle(half, d, s):
+            i = sem_i(half, d, s)
+            o = off(half, d, s)
+            here = own.at[pl.ds(o, sub)]
+            pltpu.make_async_copy(here, here, ls.at[i]).wait()
+            there = recd.at[pl.ds(o, sub)]
+            _remote(there, there, ds_.at[i], dr.at[i], partner, z).wait_recv()
+            accumulate(own, o, (recd, o))
+
+        for d, s in work:
+            settle(0, d, s)
+            i = d * NS + s
+            cp = _remote(own.at[pl.ds(off(0, d, s), sub)], recy.at[pl.ds(d * blk + s * sub, sub)],
+                         ys.at[i], yr.at[i], across, z)
+            cp.start()
+            sends.append(cp)
+        for d, s in work:
+            settle(1, d, s)
+
+        for d, s in work:
+            i = d * NS + s
+            v = d * blk + s * sub
+            there = recy.at[pl.ds(v, sub)]
+            _remote(there, there, ys.at[i], yr.at[i], across, z).wait_recv()
+            o = off(1, d, s)
+            srcs = [(recy, v)]
+            if z > 0 and d >= z:
+                there = recr.at[pl.ds(v, sub)]
+                _remote(there, there, zs.at[i], rr.at[i], ep, z).wait_recv()
+                srcs.append((recr, v))
+            if z < tps - 1 and d <= z:
+                there = recl.at[pl.ds(v, sub)]
+                _remote(there, there, zs.at[i], lr.at[i], ep, z).wait_recv()
+                srcs.append((recl, v))
+            if d != z:
+                accumulate(own, o, *srcs)
+                dst, sem, to = (recr, rr, z + 1) if d > z else (recl, lr, z - 1)
+                cp = _remote(own.at[pl.ds(o, sub)], dst.at[pl.ds(v, sub)], zs.at[i], sem.at[i], ep, to)
+                cp.start()
+                sends.append(cp)
+            else:
+                per = rows // NS
+
+                @pl.loop(0, per // 16)
+                def _(g):
+                    for cb in range(cbs):
+                        parts = []
+                        for hh in range(2):
+                            r = g * 16 * cbs + hh * 8 * cbs + cb
+                            t = own[pl.ds(o + r, 8, stride=cbs), :]
+                            for ref, s0 in srcs:
+                                t = t + ref[pl.ds(s0 + r, 8, stride=cbs), :]
+                            parts.append(t)
+                        w = jnp.concatenate(parts, axis=0).astype(jnp.bfloat16)
+                        out_ref[pl.ds(pl.multiple_of(s * per + g * 16, 16), 16), pl.ds(cb * LANES, LANES)] = w
+        for cp in sends:
+            cp.wait_send()
+
+    for z in range(tps):
+        @pl.when(tp == z)
+        def _(z=z):
+            body(z)
+
+
+def _scatter(p, rows, dim, tps):
+    blk = rows * dim // LANES
+    dma = pltpu.SemaphoreType.DMA
+    f32 = jnp.float32
+    return pl.pallas_call(
+        functools.partial(_scatter_kernel, tps),
+        out_shape=jax.ShapeDtypeStruct((rows, dim), jnp.bfloat16),
+        in_specs=[pl.BlockSpec(memory_space=pl.ANY)],
+        out_specs=pl.BlockSpec(memory_space=pltpu.VMEM),
+        scratch_shapes=[
+            pltpu.VMEM((2 * tps * blk, LANES), f32), pltpu.VMEM((2 * tps * blk, LANES), f32),
+            pltpu.VMEM((tps * blk, LANES), f32), pltpu.VMEM((tps * blk, LANES), f32),
+            pltpu.VMEM((tps * blk, LANES), f32), pltpu.VMEM((8, LANES), f32),
+            dma((2 * tps * NS,)), dma((2 * tps * NS,)), dma((2 * tps * NS,)),
+            dma((tps * NS,)), dma((tps * NS,)), dma((tps * NS,)), dma((tps * NS,)), dma((tps * NS,)),
+        ],
+        compiler_params=pltpu.CompilerParams(collective_id=1, has_side_effects=True,
+                                             vmem_limit_bytes=60 * 1024 * 1024),
+    )(p)
+
+
 def solution(mesh):
+    tps = mesh.shape['tp']
+    n_dev = tps * mesh.shape['ep']
+
     def expert_block(tok_shard, id_shard, gate_shard, w_gate, w_up, w_down):
-        x = lax.all_gather(tok_shard, GROUP_AXES, axis=0, tiled=True)
         meta = jnp.concatenate([id_shard.T.astype(jnp.float32), gate_shard.T], axis=0)
-        meta = lax.all_gather(meta, GROUP_AXES, axis=0)
+        x, meta = _gather(tok_shard, meta, n_dev, tps)
+        x = x.reshape(n_dev * tok_shard.shape[0], tok_shard.shape[1])
         choices = id_shard.shape[1]
         ids = meta[:, :choices].astype(jnp.int32)
         gates = meta[:, choices:]
         local_count = w_gate.shape[0]
         tok, gate, start = _routing(ids, gates, local_count, lax.axis_index('ep') * local_count)
         y = _moe(tok, gate, start, x, jnp.swapaxes(w_gate, 1, 2), jnp.swapaxes(w_up, 1, 2), w_down)
-        y = lax.psum_scatter(y, GROUP_AXES, scatter_dimension=0, tiled=True)
-        return y.reshape(tok_shard.shape).astype(jnp.bfloat16)
+        return _scatter(y, *tok_shard.shape, tps)
 
     return jax.shard_map(
         expert_block,

time: 373 us -> 270 us (0.72)
  waiting for transfers between devices: 210 us -> 0 us
  Pallas kernels: 99.2 us -> 256 us
  blocking collectives: 36.5 us -> 0 us
  between operations: 13.4 us -> 0.05 us
    reduce_scatter x1 -> x0, waiting for transfers between devices: 175 us -> none  [expert_block(): y = lax.psum_scatter(y, GROUP_AXES, scatter_dimension=0, tiled=True)]
    pallas_call x0 -> x2, Pallas kernels: none -> 157 us  [the longest x1 97.2 us: _scatter(): pl.pallas_call(functools.partial(_scatter_kernel, tps), out_shape=jax.Sha...]
    all_gather x1 -> x0, blocking collectives: 36.5 us -> none  [expert_block(): meta = lax.all_gather(meta, GROUP_AXES, axis=0)]
    all_gather x1 -> x0, waiting for transfers between devices: 35.1 us -> none  [expert_block(): x = lax.all_gather(tok_shard, GROUP_AXES, axis=0, tiled=True)]
  transfers between devices with their start and end apart: 2 -> 0, of which waited for: 2 -> 0; matrix products, arithmetic and copies ran while one was open for 3% -> 0% of each run, Pallas kernels for 0% -> 0%
where the time goes in v2:
time: 270 us
  Pallas kernels  256 us (95%)
  other arithmetic  9.59 us (4%)
  local copies, waits for them, and re-layouts  3.53 us (1%)
    pallas_call x1, Pallas kernels, _moe(): pl.pallas_call(functools.partial(_moe_kernel, n_tok, dim, ffp, n_exp, tok...  98.9 us
    pallas_call x1, Pallas kernels, _scatter(): pl.pallas_call(functools.partial(_scatter_kernel, tps), out_shape=jax.Sha...  97.2 us
    pallas_call x1, Pallas kernels, _gather(): pl.pallas_call(functools.partial(_gather_kernel, tps), out_shape=(jax.Sha...  60.3 us
    sort x1, other arithmetic, _routing(): lax.sort((key, gates.reshape(-1)), num_keys=1, is_stable=False)  6.45 us

profile of v2, /device:TPU:0, one launch (start us, length us, event | category | flops | bytes accessed | tf_op | source)
XLA Modules:
  0.0 269.6 jit_solution(11803600336476100969)
XLA Ops:
  0.0 0.7 convert_bitcast_fusion
  0.7 0.7 pad_maximum_fusion.meta_ref
  1.4 0.0 copy-start
  1.4 1.0 copy-done
  2.4 60.3 %shard_map.64 = (bf16[16,128,2048]{2,1,0:T(8,128)(2,1)}, f32[16,16,128]{2,1,0:T(8,128)S(1)}) custom-call(bf16[128,2048]{1,0:T(8,128)(2,1)S(1)} %copy-done, f32[16,128]{1,0:T(8,128)S(1)} %pad_maximum_fusion.meta_ref), custom_call_target="tpu_custom_call" | custom-call | tf_op jit(solution)/shard_map/pallas_call | solution.py:310
  62.7 0.1 select_bitcast_fusion
  62.8 1.1 convert_reduce_fusion.start_ref
  63.9 6.4 %sort.15 = (s32[16384]{0:T(1024)S(1)}, f32[16384]{0:T(1024)S(1)}) sort(s32[16384]{0:T(1024)S(1)} %select_bitcast_fusion, f32[16384]{0:T(1024)S(1)} %slice_bitcast_fusion), dimensions={0}, to_apply=%region_0.1 | sort | flops 229376 | bytes 262144 | tf_op jit(solution)/shard_map/sort | solution.py:183
  70.3 0.6 slice_and_fusion.tok_ref
  70.9 0.6 slice.15.gate_ref
  71.5 98.9 %shard_map.65.p_hbm = f32[32768,128]{1,0:T(8,128)} custom-call(s32[4288]{0:T(1024)} %slice_and_fusion.tok_ref, f32[4288]{0:T(1024)} %slice.15.gate_ref, s32[33]{0:T(128)} %convert_reduce_fusion.start_ref, bf16[2048,2048]{1,0:T(8,128)(2,1)} %bitcast.12, bf16[32,192,2048]{2,1,0:T(8,128)(2,1)} %bitcast.10, bf16[32,192,2048]{2,1,0:T(8,128)(2,1)} %bitcast.11, ...), custom_call_target="tpu_custom_call" | custom-call | flops 20000000000 | bytes 100000000 | tf_op jit(solution)/shard_map/pallas_call | solution.py:149
  170.5 97.2 %shard_map.66 = bf16[128,2048]{1,0:T(8,128)(2,1)} custom-call(f32[32768,128]{1,0:T(8,128)} %shard_map.65.p_hbm), custom_call_target="tpu_custom_call" | custom-call | tf_op jit(solution)/shard_map/pallas_call | solution.py:455
  267.7 1.9 copy.8
  (3 shorter events, 0.0 us)
Async XLA Ops:
  1.4 1.0 copy-start

commit v3 on v2

--- a/solution.py
+++ b/solution.py
@@ -9,23 +9,28 @@
 
 TOKEN_AXES = ('dp', 'ep', 'tp')
 GROUP_AXES = ('ep', 'tp')
-MB = 192
+MB = 160
 NBUF = 4
 LANES = 128
-
-
-def _moe_kernel(n_tok, dim, ffp, n_exp, n_pairs,
-                tok_ref, gate_ref, start_ref, x_hbm, wg_hbm, wu_hbm, w2_hbm, y_hbm,
-                xf, xst, yacc, wbuf, w2buf, xe, xb, obuf, xsem, wsem, ysem):
+LAG = 3
+
+
+def _moe_kernel(n_tok, dim, ffp, n_exp, max_blk,
+                src_ref, dst_ref, gate_ref, start_ref, x_hbm, wg_hbm, wu_hbm, w2_hbm, y_hbm,
+                xf, xst, yacc, wbuf, w2buf, xe, xb0, xb1, h0, h1, o0, o1,
+                b_exp, b_base, b_n, b_first, xsem, wsem, ysem):
     cbs = dim // LANES
     tile_rows = cbs * 8
     xc = xst.shape[1]
     n_xc = n_tok // xc
-
-    def w_copies(e, slot):
+    xb, hb, ob = (xb0, xb1), (h0, h1), (o0, o1)
+
+    def w13(e, slot):
         return (pltpu.make_async_copy(wg_hbm.at[e], wbuf.at[slot, pl.ds(0, ffp)], wsem.at[slot, 0]),
-                pltpu.make_async_copy(wu_hbm.at[e], wbuf.at[slot, pl.ds(ffp, ffp)], wsem.at[slot, 1]),
-                pltpu.make_async_copy(w2_hbm.at[e], w2buf.at[slot], wsem.at[slot, 2]))
+                pltpu.make_async_copy(wu_hbm.at[e], wbuf.at[slot, pl.ds(ffp, ffp)], wsem.at[slot, 1]))
+
+    def w2(e, slot):
+        return (pltpu.make_async_copy(w2_hbm.at[e], w2buf.at[slot], wsem.at[slot, 2]),)
 
     def x_copy(i, slot):
         return pltpu.make_async_copy(x_hbm.at[pl.ds(i * xc, xc)], xst.at[slot], xsem.at[slot])
@@ -33,8 +38,33 @@
     x_copy(0, 0).start()
     x_copy(1, 1).start()
     for e in range(NBUF - 1):
-        for c in w_copies(e, e):
+        for c in w13(e, e) + w2(e, e):
             c.start()
+
+    def clear(i, carry):
+        b_exp[i] = n_exp - 1
+        b_base[i] = 0
+        b_n[i] = 0
+        b_first[i] = 0
+        return carry
+
+    lax.fori_loop(0, max_blk, clear, 0)
+
+    def plan(e, at):
+        first, last = start_ref[e], start_ref[e + 1]
+        pieces = jnp.maximum((last - first + MB - 1) // MB, 1)
+
+        def piece(b, carry):
+            b_exp[at + b] = e
+            b_base[at + b] = first + b * MB
+            b_n[at + b] = jnp.minimum(last - first - b * MB, MB)
+            b_first[at + b] = (b == 0).astype(jnp.int32)
+            return carry
+
+        lax.fori_loop(0, pieces, piece, 0)
+        return at + pieces
+
+    end = lax.fori_loop(0, n_exp, plan, LAG)
 
     zero = jnp.zeros((tile_rows, LANES), jnp.float32)
 
@@ -62,114 +92,113 @@
 
     lax.fori_loop(0, n_xc, x_chunk, 0)
 
-    def expert(e, carry):
-        slot = lax.rem(e, NBUF)
-
-        @pl.when(e + NBUF - 1 < n_exp)
+    def step(i, q):
+        j1, j2, j3 = i - 1, i - 2, i - 3
+        e1, e2 = b_exp[j1], b_exp[j2]
+        s1, s2 = lax.rem(e1, NBUF), lax.rem(e2, NBUF)
+
+        @pl.when(b_first[j1] == 1)
         def _():
-            for c in w_copies(e + NBUF - 1, lax.rem(e + NBUF - 1, NBUF)):
-                c.start()
-
-        first = start_ref[e]
-        last = start_ref[e + 1]
-        for c in w_copies(e, slot):
-            c.wait()
-
-        def block(b, carry2):
-            base = first + b * MB
-            n = jnp.minimum(last - base, MB)
-            groups = (n + 7) // 8
-
-            def gather(m, c3):
-                row = pl.multiple_of(m * tile_rows, tile_rows)
-                vals = []
-                for k in range(8):
-                    t = tok_ref[base + m * 8 + k]
-                    src = (t >> 3) * tile_rows + (t & 7)
-                    vals.append(xf[pl.ds(src, cbs, stride=8), :])
-                for k in range(8):
-                    xe[pl.ds(row + k, cbs, stride=8), :] = vals[k]
-                return c3
-
-            lax.fori_loop(0, groups, gather, 0)
-
-            def conv(r, c3):
-                row = pl.multiple_of(r * 2 * tile_rows, 2 * tile_rows)
-                for cb in range(cbs):
-                    v = jnp.concatenate([xe[pl.ds(row + cb * 8, 8), :],
-                                         xe[pl.ds(row + tile_rows + cb * 8, 8), :]], axis=0)
-                    xb[pl.ds(pl.multiple_of(r * 16, 16), 16), pl.ds(cb * LANES, LANES)] = v.astype(jnp.bfloat16)
-                return c3
-
-            lax.fori_loop(0, (n + 15) // 16, conv, 0)
-
-            at = lax.dot_general(wbuf[slot], xb[...], (((1,), (1,)), ((), ())),
-                                 preferred_element_type=jnp.float32)
-            ht = jax.nn.silu(at[:ffp]) * at[ffp:]
-            h = ht.T.astype(jnp.bfloat16)
-            for nc in range(dim // 256):
-                o = jnp.dot(h, w2buf[slot, :, pl.ds(nc * 256, 256)], preferred_element_type=jnp.float32)
-                for rb in range(MB // 8):
-                    for s in range(2):
-                        obuf[pl.ds(rb * tile_rows + (nc * 2 + s) * 8, 8), :] = (
-                            o[rb * 8:rb * 8 + 8, s * LANES:(s + 1) * LANES])
-
-            def combine(m, c3):
-                row = pl.multiple_of(m * tile_rows, tile_rows)
+            for c in w13(e1, s1):
+                c.wait()
+
+            @pl.when(e1 + NBUF - 1 < n_exp)
+            def _():
+                for c in w13(e1 + NBUF - 1, lax.rem(e1 + NBUF - 1, NBUF)):
+                    c.start()
+
+        @pl.when(b_first[j2] == 1)
+        def _():
+            for c in w2(e2, s2):
+                c.wait()
+
+            @pl.when(e2 + NBUF - 1 < n_exp)
+            def _():
+                for c in w2(e2 + NBUF - 1, lax.rem(e2 + NBUF - 1, NBUF)):
+                    c.start()
+
+        base0, base3, n3 = b_base[i], b_base[j3], b_n[j3]
+
+        at = lax.dot_general(wbuf[s1], xb[1 - q][...], (((1,), (1,)), ((), ())),
+                             preferred_element_type=jnp.float32)
+
+        h = hb[q][...]
+        for nc in range(dim // 256):
+            o = jnp.dot(h, w2buf[s2, :, pl.ds(nc * 256, 256)], preferred_element_type=jnp.float32)
+            for rb in range(MB // 8):
+                for s in range(2):
+                    ob[q][pl.ds(rb * tile_rows + (nc * 2 + s) * 8, 8), :] = (
+                        o[rb * 8:rb * 8 + 8, s * LANES:(s + 1) * LANES])
+
+        for g in range(MB // 16):
+            vals = [xf[pl.ds(src_ref[base0 + g * 16 + k], cbs, stride=8), :] for k in range(16)]
+            for k in range(16):
+                xe[pl.ds((g * 2 + k // 8) * tile_rows + k % 8, cbs, stride=8), :] = vals[k]
+            for cb in range(cbs):
+                v = jnp.concatenate([xe[pl.ds(g * 2 * tile_rows + cb * 8, 8), :],
+                                     xe[pl.ds((g * 2 + 1) * tile_rows + cb * 8, 8), :]], axis=0)
+                xb[q][pl.ds(g * 16, 16), pl.ds(cb * LANES, LANES)] = v.astype(jnp.bfloat16)
+            for m in range(2 * g, 2 * g + 2):
                 dst, acc = [], []
                 for k in range(8):
                     p = m * 8 + k
-                    t = jnp.where(p < n, tok_ref[base + p], n_tok)
-                    d = pl.multiple_of(t * cbs, cbs)
+                    d = pl.multiple_of(jnp.where(p < n3, dst_ref[base3 + p], n_tok * cbs), cbs)
                     dst.append(d)
                     acc.append(yacc[pl.ds(d, cbs), :]
-                               + obuf[pl.ds(row + k, cbs, stride=8), :] * gate_ref[base + p])
+                               + ob[1 - q][pl.ds(m * tile_rows + k, cbs, stride=8), :] * gate_ref[base3 + p])
                 for k in range(8):
                     yacc[pl.ds(dst[k], cbs), :] = acc[k]
-                return c3
-
-            lax.fori_loop(0, groups, combine, 0)
-            return carry2
-
-        lax.fori_loop(0, (last - first + MB - 1) // MB, block, 0)
+
+        ht = jax.nn.silu(at[:ffp]) * at[ffp:]
+        hb[1 - q][...] = ht.T.astype(jnp.bfloat16)
+
+    def pair(t, carry):
+        step(LAG + 2 * t, 0)
+        step(LAG + 2 * t + 1, 1)
         return carry
 
-    lax.fori_loop(0, n_exp, expert, 0)
+    lax.fori_loop(0, (end + 1) // 2, pair, 0)
     out = pltpu.make_async_copy(yacc.at[pl.ds(0, n_tok * cbs)], y_hbm, ysem)
     out.start()
     out.wait()
 
 
-def _moe(tok, gate, start, x, wgt, wut, w2):
+def _moe(src, dst, gate, start, x, wgt, wut, w2):
     n_exp, ffp, dim = wgt.shape
     n_tok = x.shape[0]
     cbs = dim // LANES
+    n_pairs = src.shape[0] - MB
+    max_blk = n_exp + n_pairs // MB + 2 * LAG + 4
     smem = pl.BlockSpec(memory_space=pltpu.SMEM)
     hbm = pl.BlockSpec(memory_space=pl.ANY)
+    f32, bf16 = jnp.float32, jnp.bfloat16
     return pl.pallas_call(
-        functools.partial(_moe_kernel, n_tok, dim, ffp, n_exp, tok.shape[0]),
+        functools.partial(_moe_kernel, n_tok, dim, ffp, n_exp, max_blk),
         out_shape=jax.ShapeDtypeStruct((n_tok * cbs, LANES), jnp.float32),
-        in_specs=[smem, smem, smem, hbm, hbm, hbm, hbm],
+        in_specs=[smem, smem, smem, smem, hbm, hbm, hbm, hbm],
         out_specs=hbm,
         scratch_shapes=[
-            pltpu.VMEM((n_tok * cbs, LANES), jnp.float32),
-            pltpu.VMEM((2, 128, dim), jnp.bfloat16),
-            pltpu.VMEM(((n_tok + 8) * cbs, LANES), jnp.float32),
-            pltpu.VMEM((NBUF, 2 * ffp, dim), jnp.bfloat16),
-            pltpu.VMEM((NBUF, ffp, dim), jnp.bfloat16),
-            pltpu.VMEM((MB * cbs, LANES), jnp.float32),
-            pltpu.VMEM((MB, dim), jnp.bfloat16),
-            pltpu.VMEM((MB * cbs, LANES), jnp.float32),
+            pltpu.VMEM((n_tok * cbs, LANES), f32),
+            pltpu.VMEM((2, 128, dim), bf16),
+            pltpu.VMEM(((n_tok + 8) * cbs, LANES), f32),
+            pltpu.VMEM((NBUF, 2 * ffp, dim), bf16),
+            pltpu.VMEM((NBUF, ffp, dim), bf16),
+            pltpu.VMEM((MB * cbs, LANES), f32),
+            pltpu.VMEM((MB, dim), bf16), pltpu.VMEM((MB, dim), bf16),
+            pltpu.VMEM((MB, ffp), bf16), pltpu.VMEM((MB, ffp), bf16),
+            pltpu.VMEM((MB * cbs, LANES), f32), pltpu.VMEM((MB * cbs, LANES), f32),
+            pltpu.SMEM((max_blk,), jnp.int32), pltpu.SMEM((max_blk,), jnp.int32),
+            pltpu.SMEM((max_blk,), jnp.int32), pltpu.SMEM((max_blk,), jnp.int32),
             pltpu.SemaphoreType.DMA((2,)),
             pltpu.SemaphoreType.DMA((NBUF, 3)),
             pltpu.SemaphoreType.DMA,
         ],
         compiler_params=pltpu.CompilerParams(vmem_limit_bytes=62 * 1024 * 1024),
         cost_estimate=pl.CostEstimate(flops=20_000_000_000, bytes_accessed=100_000_000, transcendentals=1_000_000),
-    )(tok, gate, start, x, wgt, wut, w2)
-
-
-def _routing(ids, gates, local_count, first_expert):
+    )(src, dst, gate, start, x, wgt, wut, w2)
+
+
+def _routing(ids, gates, local_count, first_expert, cbs):
     devs, choices, rows = ids.shape
     n_tok = devs * rows
     tok = (lax.broadcasted_iota(jnp.int32, ids.shape, 0) * rows
@@ -182,7 +211,8 @@
     start = jnp.sum((key[None, :] < bounds[:, None]).astype(jnp.int32), axis=1)
     key_s, gate_s = lax.sort((key, gates.reshape(-1)), num_keys=1, is_stable=False)
     tok_s = key_s[:n_pairs + MB] & (n_tok - 1)
-    return tok_s, gate_s[:n_pairs + MB], start
+    src = (tok_s >> 3) * (8 * cbs) + (tok_s & 7)
+    return src, tok_s * cbs, gate_s[:n_pairs + MB], start
 
 
 def _wire(ep, tp):
@@ -481,8 +511,9 @@
         ids = meta[:, :choices].astype(jnp.int32)
         gates = meta[:, choices:]
         local_count = w_gate.shape[0]
-        tok, gate, start = _routing(ids, gates, local_count, lax.axis_index('ep') * local_count)
-        y = _moe(tok, gate, start, x, jnp.swapaxes(w_gate, 1, 2), jnp.swapaxes(w_up, 1, 2), w_down)
+        src, dst, gate, start = _routing(ids, gates, local_count, lax.axis_index('ep') * local_count,
+                                         tok_shard.shape[1] // LANES)
+        y = _moe(src, dst, gate, start, x, jnp.swapaxes(w_gate, 1, 2), jnp.swapaxes(w_up, 1, 2), w_down)
         return _scatter(y, *tok_shard.shape, tps)
 
     return jax.shard_map(

time: 270 us -> 240 us (0.89)
  Pallas kernels: 256 us -> 226 us
    pallas_call x1, Pallas kernels: 98.9 us -> 69.2 us  [_moe(): pl.pallas_call(functools.partial(_moe_kernel, n_tok, dim, ffp, n_exp, max...]
where the time goes in v3:
time: 240 us
  Pallas kernels  226 us (94%)
  other arithmetic  9.63 us (4%)
  local copies, waits for them, and re-layouts  3.53 us (1%)
    pallas_call x1, Pallas kernels, _scatter(): pl.pallas_call(functools.partial(_scatter_kernel, tps), out_shape=jax.Sha...  97 us
    pallas_call x1, Pallas kernels, _moe(): pl.pallas_call(functools.partial(_moe_kernel, n_tok, dim, ffp, n_exp, max...  69.2 us
    pallas_call x1, Pallas kernels, _gather(): pl.pallas_call(functools.partial(_gather_kernel, tps), out_shape=(jax.Sha...  60.3 us
    sort x1, other arithmetic, _routing(): lax.sort((key, gates.reshape(-1)), num_keys=1, is_stable=False)  6.45 us

profile of v3, /device:TPU:0, one launch (start us, length us, event | category | flops | bytes accessed | tf_op | source)
XLA Modules:
  0.0 239.6 jit_solution(3653765067678521865)
XLA Ops:
  0.0 0.7 convert_bitcast_fusion
  0.7 0.7 pad_maximum_fusion.meta_ref
  1.4 0.0 copy-start
  1.4 1.0 copy-done
  2.4 60.3 %shard_map.64 = (bf16[16,128,2048]{2,1,0:T(8,128)(2,1)}, f32[16,16,128]{2,1,0:T(8,128)S(1)}) custom-call(bf16[128,2048]{1,0:T(8,128)(2,1)S(1)} %copy-done, f32[16,128]{1,0:T(8,128)S(1)} %pad_maximum_fusion.meta_ref), custom_call_target="tpu_custom_call" | custom-call | tf_op jit(solution)/shard_map/pallas_call | solution.py:340
  62.7 0.1 select_bitcast_fusion
  62.8 1.1 convert_reduce_fusion.start_ref
  63.9 6.4 %sort.15 = (s32[16384]{0:T(1024)S(1)}, f32[16384]{0:T(1024)S(1)}) sort(s32[16384]{0:T(1024)S(1)} %select_bitcast_fusion, f32[16384]{0:T(1024)S(1)} %slice_bitcast_fusion), dimensions={0}, to_apply=%region_0.1 | sort | flops 229376 | bytes 262144 | tf_op jit(solution)/shard_map/sort | solution.py:212
  70.4 0.6 fusion
  71.0 0.6 slice.15.gate_ref
  71.6 69.2 %shard_map.65.p_hbm = f32[32768,128]{1,0:T(8,128)} custom-call(s32[4256]{0:T(1024)} %get-tuple-element.14.src_ref, s32[4256]{0:T(1024)} %get-tuple-element.13.dst_ref, f32[4256]{0:T(1024)} %slice.15.gate_ref, s32[33]{0:T(128)} %convert_reduce_fusion.start_ref, bf16[2048,2048]{1,0:T(8,128)(2,1)} %bitcast.12, bf16[32,192,2048]{2,1,0:T(8,128)(2,1)} %bitcast.10, ...), custom_call_target="tpu_custom_call" | custom-call | flops 20000000000 | bytes 100000000 | tf_op jit(solution)/shard_map/pallas_call | solution.py:175
  140.8 97.0 %shard_map.66 = bf16[128,2048]{1,0:T(8,128)(2,1)} custom-call(f32[32768,128]{1,0:T(8,128)} %shard_map.65.p_hbm), custom_call_target="tpu_custom_call" | custom-call | tf_op jit(solution)/shard_map/pallas_call | solution.py:485
  237.8 1.9 copy.8
  (3 shorter events, 0.0 us)
Async XLA Ops:
  1.4 1.0 copy-start
